TPU v7x, 32 devices: a whole 2x2x4 slice. The times are simulated.
32 devices in a mesh: mem: 8 (over y, x, core), pix: 4 (over z).
Axes of the slice: x: 2, y: 2, z: 4, core: 2. Of those that a mesh axis runs over, the one named last changes fastest.
Arguments:
- prior_motion: bfloat16 [64, 16, 131072], P('mem', None, 'pix'), may hold values from -6 to 6
- measured_motion: float32 [1200], replicated, may hold values from -1.6 to 1.6
- measurement_noise_stddev: float32 [1200], replicated, may hold values from 0.05 to 0.5
- gaussian_jitter: float32 [2, 1200, 64], replicated, may hold values from -6 to 6
- scene_couples: int32 [2, 1200], replicated, may hold values from 0 to 15, as said below
- targeted_tile_number: int32 [1200], replicated, may hold values from 0 to 2047
Outputs:
- analysis: bfloat16 [64, 16, 131072], P('mem', None, 'pix')
Inputs may be any that keep to these rules, and one draw needn't show every extreme that they name: scene_couples[0, k] < scene_couples[1, k]: row 0 holds the earlier acquisition, row 1 the later.
All inputs are finite; a program needn't handle non-finite values.
Results may differ from a plain program's by a relative error of at most 0.011.
Values may be sent and summed in bfloat16 or wider, within the bound.
A program may use at most 192 MiB of HBM per device.

v0:
```python
import math
import jax
import jax.numpy as jnp
from jax import lax
from jax.sharding import PartitionSpec as P

BLK = 64
PASS_COUNT = 2


def block_sums(pieces):
    part_cells = pieces.shape[2]
    block_count = part_cells // BLK
    summer = (
        jnp.arange(part_cells, dtype=jnp.int32)[:, None] // BLK
        == jnp.arange(block_count, dtype=jnp.int32)[None, :]
    ).astype(jnp.bfloat16)
    flat = jnp.dot(pieces.reshape(-1, part_cells), summer, preferred_element_type=jnp.float32)
    return flat.reshape(pieces.shape[0], pieces.shape[1], block_count)


def with_sums(pieces):
    return (pieces, block_sums(pieces))


def to_pixels(ground_motion_vector):
    return with_sums(
        lax.all_to_all(ground_motion_vector, "mem", split_axis=2, concat_axis=0, tiled=True)
    )


def to_members(pixel_state):
    return lax.all_to_all(pixel_state, "mem", split_axis=0, concat_axis=2, tiled=True)


def predict(sums, picker):
    flat_sums = sums.reshape(sums.shape[0], -1)
    return (
        jnp.dot(
            picker, flat_sums.T, precision=lax.Precision.HIGHEST, preferred_element_type=jnp.float32
        )
        / BLK
    )


def member_terms(predicted, measured_motion, member_anomaly, noise):
    realization_vectors = predicted.shape[1]
    centred = predicted - jnp.mean(predicted, axis=1, keepdims=True)
    scaled = centred / (member_anomaly[:, None] * math.sqrt(realization_vectors - 1))
    misfit = (
        measured_motion[:, None] + member_anomaly[:, None] * noise - predicted
    ) / member_anomaly[:, None]
    return (scaled, misfit)


def products(scaled, misfit):
    gram = jnp.dot(
        scaled.T, scaled, precision=lax.Precision.HIGHEST, preferred_element_type=jnp.float32
    )
    cross = jnp.dot(
        scaled.T, misfit, precision=lax.Precision.HIGHEST, preferred_element_type=jnp.float32
    )
    return (gram, cross)


def solve_mixing(gram, cross):
    realization_vectors = gram.shape[0]
    factor = jnp.linalg.cholesky(jnp.eye(realization_vectors, dtype=jnp.float32) + gram)
    return (
        jax.scipy.linalg.cho_solve((factor, True), cross) / math.sqrt(realization_vectors - 1)
    ).astype(jnp.bfloat16)


def update(pixel_state, mixing):
    realization_vectors = pixel_state.shape[0]
    average = jnp.sum(pixel_state, axis=0, dtype=jnp.float32) / realization_vectors
    anomaly = (pixel_state.astype(jnp.float32) - average).astype(jnp.bfloat16)
    change = jnp.dot(
        mixing.T, anomaly.reshape(realization_vectors, -1), preferred_element_type=jnp.float32
    )
    return (pixel_state.astype(jnp.float32) + change.reshape(pixel_state.shape)).astype(
        jnp.bfloat16
    )


def body(
    prior_motion,
    measured_motion,
    measurement_noise_stddev,
    gaussian_jitter,
    scene_couples,
    targeted_tile_number,
):
    cells_per_tile = prior_motion.shape[2]
    part_width = cells_per_tile // lax.axis_size("mem")
    local_blocks = part_width // BLK
    first_block = (
        lax.axis_index("pix") * cells_per_tile + lax.axis_index("mem") * part_width
    ) // BLK
    block_range = first_block + jnp.arange(local_blocks, dtype=jnp.int32)
    block_table = (targeted_tile_number[:, None] == block_range[None, :]).astype(jnp.float32)
    scene_timeline = jnp.arange(prior_motion.shape[1], dtype=jnp.int32)
    pair_table = (scene_timeline[None, :] == scene_couples[1][:, None]).astype(jnp.float32) - (
        scene_timeline[None, :] == scene_couples[0][:, None]
    ).astype(jnp.float32)
    picker = (pair_table[:, :, None] * block_table[:, None, :]).reshape(pair_table.shape[0], -1)
    member_anomaly = jnp.sqrt(jnp.float32(float(PASS_COUNT))) * measurement_noise_stddev
    pixel_state, sums = to_pixels(prior_motion)
    for iteration in range(PASS_COUNT):
        if iteration > 0:
            sums = block_sums(pixel_state)
        predicted = predict(sums, picker)
        predicted = lax.psum(predicted, ("mem", "pix"))
        scaled, misfit = member_terms(
            predicted, measured_motion, member_anomaly, gaussian_jitter[iteration]
        )
        gram, cross = products(scaled, misfit)
        pixel_state = update(pixel_state, solve_mixing(gram, cross))
    return to_members(pixel_state)


def solution(mesh):
    return jax.shard_map(
        body,
        mesh=mesh,
        in_specs=(P("mem", None, "pix"), P(), P(), P(), P(), P()),
        out_specs=P("mem", None, "pix"),
        check_vma=False,
    )
```

profile of v0, /device:TPU:8, one launch (start us, length us, event | category | flops | bytes accessed | tf_op | source)
XLA Modules:
  0.0 957.3 jit_solution(7385386645052010220)
XLA Ops:
  6.5 52.6 %copy.41 = bf16[8,16,32768]{1,0,2:T(8,128)(2,1)} copy(bf16[8,16,32768]{2,1,0:T(8,128)(2,1)} %param.9) | data formatting | bytes 16777216 | tf_op args[0]
  59.1 103.9 %reshape.195 = bf16[8,2,262144]{2,1,0:T(2,128)(2,1)} reshape(bf16[32768,8,16]{2,1,0:T(8,128)(2,1)} %bitcast.86) | data formatting | bytes 16777216
  171.8 90.4 %all-to-all-done = bf16[8,2,262144]{2,1,0:T(2,128)(2,1)} async-done(((bf16[8,2,262144]{2,1,0:T(2,128)(2,1)}), bf16[8,2,262144]{2,1,0:T(2,128)(2,1)}, u32[]{:S(2)}, u32[]{:S(2)}) %all-to-all-start) | async-done | bytes 8388640 | tf_op jit(solution)/shard_map/all_to_all | solution.py:28
  262.2 80.3 %reshape.196 = bf16[32768,8,16]{2,1,0:T(8,128)(2,1)} reshape(bf16[8,2,262144]{2,1,0:T(2,128)(2,1)} %all-to-all-done) | data formatting | bytes 16777216
  342.5 52.2 %copy.65 = bf16[8,16,8,4096]{3,2,1,0:T(8,128)(2,1)} copy(bf16[8,16,8,4096]{1,0,3,2:T(8,128)(2,1)} %bitcast) | data formatting | bytes 16777216 | tf_op jit(solution)/shard_map/all_to_all | solution.py:28
  394.7 11.4 %bitcast_convert_fusion = f32[8,8,16,4096]{3,0,2,1:T(8,128)} fusion(bf16[8,16,8,4096]{3,2,1,0:T(8,128)(2,1)} %copy.65), kind=kLoop, calls=%fused_computation.14 | loop fusion | flops 4194304 | bytes 25165824 | tf_op jit(solution)/shard_map/convert_element_type | solution.py:81
  406.1 5.2 fusion.8
  411.3 60.0 %copy.44 = bf16[8,8,16,4096]{3,2,1,0:T(8,128)(2,1)} copy(bf16[8,8,16,4096]{2,1,3,0:T(8,128)(2,1)} %bitcast.4) | data formatting | bytes 16777216 | tf_op jit(solution)/shard_map/all_to_all | solution.py:28
  471.3 6.5 convolution_bitcast_fusion
  478.2 6.6 convolution_multiply_fusion.1
  484.9 15.2 %copy.90 = f32[8,8,16,4096]{3,2,1,0:T(8,128)S(1)} copy(f32[8,8,16,4096]{3,0,2,1:T(8,128)} %bitcast_convert_fusion) | data formatting | bytes 33554432 | tf_op jit(solution)/shard_map/convert_element_type | solution.py:81
  500.1 10.9 %copy.73 = f32[8,8,16,4096]{3,1,2,0:T(8,128)S(1)} copy(f32[8,8,16,4096]{3,2,1,0:T(8,128)S(1)} %copy.90) | data formatting | bytes 33554432
  515.0 98.2 %all-reduce.3.cloned.1.call-done = f32[1200,64]{0,1:T(8,128)} async-done(((f32[1200,64]{0,1:T(8,128)}), f32[1200,64]{0,1:T(8,128)}) %all-reduce.3.cloned.1.call-update) | async-done | bytes 307216 | tf_op jit(solution)/shard_map/psum | solution.py:113
  615.9 5.8 cholesky.44
  630.1 21.8 %convert_reduce_fusion = (f32[16,4096]{1,0:T(8,128)S(1)}, bf16[64,16,4096]{2,0,1:T(8,128)(2,1)}) fusion(bf16[64,64,1]{1,0,2:T(8,128)(2,1)S(1)} %fusion.14, bf16[8,16,8,4096]{3,2,1,0:T(8,128)(2,1)} %bitcast.113, f32[8,8,16,4096]{3,0,2,1:T(8,128)} %bitcast_convert_fusion), kind=kOutput, calls=%fused_computation.2 | convolution fusion | flops 553582592 | bytes 33824768 | tf_op jit(solution)/shard_map/dot_general | solution.py:78
  651.9 11.4 %copy.51 = bf16[64,16,4096]{2,1,0:T(8,128)(2,1)} copy(bf16[64,16,4096]{2,0,1:T(8,128)(2,1)} %get-tuple-element.12) | data formatting | bytes 16777216 | tf_op jit(solution)/shard_map/convert_element_type | solution.py:81
  663.2 5.8 fusion.9
  669.2 6.6 convolution_multiply_fusion
  675.9 128.1 %all-reduce.5.cloned.1.call-done = f32[1200,64]{0,1:T(8,128)} async-done(((f32[1200,64]{0,1:T(8,128)}), f32[1200,64]{0,1:T(8,128)}) %all-reduce.5.cloned.1.call-update) | async-done | bytes 307216 | tf_op jit(solution)/shard_map/psum | solution.py:113
  806.6 5.8 cholesky.55
  820.8 10.6 %fusion.1 = bf16[64,16,4096]{2,0,1:T(8,128)(2,1)} fusion(bf16[64,16,4096]{2,0,1:T(8,128)(2,1)} %get-tuple-element.12, bf16[64,64,1]{1,0,2:T(8,128)(2,1)S(1)} %fusion.13, f32[16,4096]{1,0:T(8,128)S(1)} %broadcast_multiply_fusion.1), kind=kOutput, calls=%fused_computation.4 | convolution fusion | flops 562036736 | bytes 17047552 | tf_op jit(solution)/shard_map/dot_general | solution.py:78
  831.4 11.2 %copy.58 = bf16[64,16,4096]{2,1,0:T(8,128)(2,1)} copy(bf16[64,16,4096]{2,0,1:T(8,128)(2,1)} %fusion.1) | data formatting | bytes 16777216 | tf_op jit(solution)/shard_map/convert_element_type | solution.py:81
  842.6 99.7 %all_to_all.33 = bf16[64,16,4096]{2,1,0:T(8,128)(2,1)} all-to-all(bf16[64,16,4096]{2,1,0:T(8,128)(2,1)} %copy.58), channel_id=1, replica_groups=mesh['mem'=8,'pix'=4] {'mem'}, dimensions={0} | all-to-all | bytes 16777216 | tf_op jit(solution)/shard_map/all_to_all | solution.py:33
  942.3 7.9 copy.72
  (53 shorter events, 35.0 us)
Async XLA Ops:
  163.1 5.7 copy-start
  163.1 5.7 copy-start.1
  163.1 5.7 copy-start.2
  163.1 99.1 %all-to-all-start = ((bf16[8,2,262144]{2,1,0:T(2,128)(2,1)}), bf16[8,2,262144]{2,1,0:T(2,128)(2,1)}, u32[]{:S(2)}, u32[]{:S(2)}) async-start(bf16[8,2,262144]{2,1,0:T(2,128)(2,1)} %reshape.195), calls=%async_computation | async-start | bytes 16777216 | tf_op jit(solution)/shard_map/all_to_all | solution.py:28
  168.2 445.1 %all-reduce.3.cloned.1.call-start = ((), (), s32[]{:S(2)}) async-start(), calls=%async_computation.2 | async-start | bytes 655360 | tf_op jit(solution)/shard_map/psum | solution.py:113
  484.9 319.1 %all-reduce.5.cloned.1.call-start = ((), (), s32[]{:S(2)}) async-start(), calls=%async_computation.3 | async-start | bytes 655360 | tf_op jit(solution)/shard_map/psum | solution.py:113
  511.1 117.0 %copy-start.3 = (f32[2,1200,64]{1,2,0:T(8,128)S(1)}, f32[2,1200,64]{1,2,0:T(8,128)}, u32[]{:S(2)}) copy-start(f32[2,1200,64]{1,2,0:T(8,128)} %param.12) | copy-start | bytes 1843204
  511.1 117.0 %copy-start.4 = (f32[1200]{0:T(1024)S(1)}, f32[1200]{0:T(1024)}, u32[]{:S(2)}) copy-start(f32[1200]{0:T(1024)} %param.10) | copy-start | bytes 14404
Sparse Core Ops, SparseCore 0:
  485.0 128.2 all-reduce.2
  676.0 127.9 all-reduce.4
where the time goes:
time: 970 us; the launch traced here: 957 us
  local copies, waits for them, and re-layouts  406 us (42%)
  waiting for transfers between devices  317 us (33%)
  blocking collectives  99.7 us (10%)
  matrix products  64.9 us (7%)
  other arithmetic  49.9 us (5%)
  between operations  13.9 us (1%)
    unnamed x15, local copies, waits for them, and re-layouts  248 us
    psum x2, waiting for transfers between devices, body(): predicted = lax.psum(predicted, ('mem', 'pix'))  226 us
    all_to_all x2, local copies, waits for them, and re-layouts, to_pixels(): lax.all_to_all(ground_motion_vector, 'mem', split_axis=2, concat_axis=0,...  112 us
    all_to_all x1, blocking collectives, to_members(): lax.all_to_all(pixel_state, 'mem', split_axis=0, concat_axis=2, tiled=True)  99.7 us
    all_to_all x1, waiting for transfers between devices, to_pixels(): lax.all_to_all(ground_motion_vector, 'mem', split_axis=2, concat_axis=0,...  90.4 us
    dot_general x2, matrix products, update(): jnp.dot(mixing.T, anomaly.reshape(realization_vectors, -1), preferred_ele...  32.4 us
    convert_element_type x2, local copies, waits for them, and re-layouts, update(): (pixel_state.astype(jnp.float32) + change.reshape(pixel_state.shape)).ast...  22.6 us
  transfers between devices with their start and end apart: 3, of which 3 were waited for; matrix products, arithmetic and copies ran while one was open for 3% of the time, Pallas kernels for 0%

commit v1 on v0

--- a/solution.py
+++ b/solution.py
@@ -6,6 +6,11 @@
 
 BLK = 64
 PASS_COUNT = 2
+
+
+def summed_here(value, axis):
+    terms = lax.all_gather(value, axis)
+    return jnp.sum(terms, axis=0)
 
 
 def block_sums(pieces):
@@ -110,7 +115,7 @@
         if iteration > 0:
             sums = block_sums(pixel_state)
         predicted = predict(sums, picker)
-        predicted = lax.psum(predicted, ("mem", "pix"))
+        predicted = summed_here(predicted, ("mem", "pix"))
         scaled, misfit = member_terms(
             predicted, measured_motion, member_anomaly, gaussian_jitter[iteration]
         )

time: 970 us -> 838 us (0.86)
  waiting for transfers between devices: 317 us -> 176 us
  other arithmetic: 49.9 us -> 59.6 us
    psum x2 -> x0, waiting for transfers between devices: 226 us -> none  [body(): predicted = lax.psum(predicted, ('mem', 'pix'))]
    all_gather x0 -> x2, waiting for transfers between devices: none -> 85.8 us  [summed_here(): terms = lax.all_gather(value, axis)]
    unnamed x15 -> x19, local copies, waits for them, and re-layouts: 248 us -> 249 us
  transfers between devices with their start and end apart: 3 -> 3, of which waited for: 3 -> 2; matrix products, arithmetic and copies ran while one was open for 3% -> 13% of each run, Pallas kernels for 0% -> 0%
where the time goes in v1:
time: 838 us; the launch traced here: 824 us
  local copies, waits for them, and re-layouts  408 us (49%)
  waiting for transfers between devices  176 us (21%)
  blocking collectives  99.7 us (12%)
  matrix products  60.2 us (7%)
  other arithmetic  59.6 us (7%)
  between operations  14.2 us (2%)
    unnamed x19, local copies, waits for them, and re-layouts  249 us
    all_to_all x2, local copies, waits for them, and re-layouts, to_pixels(): lax.all_to_all(ground_motion_vector, 'mem', split_axis=2, concat_axis=0,...  112 us
    all_to_all x1, blocking collectives, to_members(): lax.all_to_all(pixel_state, 'mem', split_axis=0, concat_axis=2, tiled=True)  99.7 us
    all_to_all x1, waiting for transfers between devices, to_pixels(): lax.all_to_all(ground_motion_vector, 'mem', split_axis=2, concat_axis=0,...  90.6 us
    all_gather x2, waiting for transfers between devices, summed_here(): terms = lax.all_gather(value, axis)  85.8 us
    dot_general x2, matrix products, update(): jnp.dot(mixing.T, anomaly.reshape(realization_vectors, -1), preferred_ele...  32.2 us
    convert_element_type x2, local copies, waits for them, and re-layouts, update(): (pixel_state.astype(jnp.float32) + change.reshape(pixel_state.shape)).ast...  22.6 us
  transfers between devices with their start and end apart: 3, of which 2 were waited for; matrix products, arithmetic and copies ran while one was open for 13% of the time, Pallas kernels for 0%

profile of v1, /device:TPU:8, one launch (start us, length us, event | category | flops | bytes accessed | tf_op | source)
XLA Modules:
  0.0 823.6 jit_solution(8260455380296624256)
XLA Ops:
  6.5 52.6 %copy.41 = bf16[8,16,32768]{1,0,2:T(8,128)(2,1)} copy(bf16[8,16,32768]{2,1,0:T(8,128)(2,1)} %param.9) | data formatting | bytes 16777216 | tf_op args[0]
  59.1 103.9 %reshape.209 = bf16[8,2,262144]{2,1,0:T(2,128)(2,1)} reshape(bf16[32768,8,16]{2,1,0:T(8,128)(2,1)} %bitcast.90) | data formatting | bytes 16777216
  163.1 5.1 all-to-all-start
  171.6 90.6 %all-to-all-done = bf16[8,2,262144]{2,1,0:T(2,128)(2,1)} async-done(((bf16[8,2,262144]{2,1,0:T(2,128)(2,1)}), bf16[8,2,262144]{2,1,0:T(2,128)(2,1)}, u32[]{:S(2)}, u32[]{:S(2)}) %all-to-all-start) | async-done | bytes 8388640 | tf_op jit(solution)/shard_map/all_to_all | solution.py:33
  262.2 80.3 %reshape.210 = bf16[32768,8,16]{2,1,0:T(8,128)(2,1)} reshape(bf16[8,2,262144]{2,1,0:T(2,128)(2,1)} %all-to-all-done) | data formatting | bytes 16777216
  342.5 60.0 %copy.44 = bf16[8,8,16,4096]{3,2,1,0:T(8,128)(2,1)} copy(bf16[8,8,16,4096]{2,1,3,0:T(8,128)(2,1)} %bitcast.4) | data formatting | bytes 16777216 | tf_op jit(solution)/shard_map/all_to_all | solution.py:33
  402.5 6.3 convolution_bitcast_fusion
  409.2 6.6 fusion.9
  416.3 52.4 %copy.65 = bf16[8,16,8,4096]{3,2,1,0:T(8,128)(2,1)} copy(bf16[8,16,8,4096]{1,0,3,2:T(8,128)(2,1)} %bitcast) | data formatting | bytes 16777216 | tf_op jit(solution)/shard_map/all_to_all | solution.py:33
  468.8 11.4 %bitcast_convert_fusion = f32[8,8,16,4096]{3,0,2,1:T(8,128)} fusion(bf16[8,16,8,4096]{3,2,1,0:T(8,128)(2,1)} %copy.65), kind=kLoop, calls=%fused_computation.14 | loop fusion | flops 4194304 | bytes 25165824 | tf_op jit(solution)/shard_map/convert_element_type | solution.py:86
  480.2 15.3 %copy.90 = f32[8,8,16,4096]{3,2,1,0:T(8,128)S(1)} copy(f32[8,8,16,4096]{3,0,2,1:T(8,128)} %bitcast_convert_fusion) | data formatting | bytes 33554432 | tf_op jit(solution)/shard_map/convert_element_type | solution.py:86
  495.6 11.7 %copy.73 = f32[8,8,16,4096]{3,1,2,0:T(8,128)} copy(f32[8,8,16,4096]{3,2,1,0:T(8,128)S(1)} %copy.90) | data formatting | bytes 33554432
  509.3 9.1 %subtract_convert_fusion = bf16[64,65536]{1,0:T(8,128)(2,1)} fusion(f32[64,65536]{1,0:T(8,128)} %bitcast.115, f32[65536]{0:T(1024)S(1)} %bitcast.122), kind=kLoop, calls=%fused_computation.8 | loop fusion | flops 8388608 | bytes 25427968 | tf_op jit(solution)/shard_map/convert_element_type | solution.py:82
  523.9 5.8 cholesky.44
  536.8 21.6 %convert_reduce_fusion = (f32[16,4096]{1,0:T(8,128)S(1)}, bf16[64,16,4096]{2,0,1:T(8,128)(2,1)}) fusion(bf16[64,64,1]{1,0,2:T(8,128)(2,1)S(1)} %fusion.16, bf16[8,16,8,4096]{3,2,1,0:T(8,128)(2,1)} %bitcast.119, f32[8,8,16,4096]{3,0,2,1:T(8,128)} %bitcast_convert_fusion), kind=kOutput, calls=%fused_computation.2 | convolution fusion | flops 553582592 | bytes 33824768 | tf_op jit(solution)/shard_map/dot_general | solution.py:83
  558.4 11.4 %copy.51 = bf16[64,16,4096]{2,1,0:T(8,128)(2,1)} copy(bf16[64,16,4096]{2,0,1:T(8,128)(2,1)} %get-tuple-element.16) | data formatting | bytes 16777216 | tf_op jit(solution)/shard_map/convert_element_type | solution.py:86
  569.7 5.8 fusion.11
  575.7 6.6 fusion.10
  582.4 85.8 %all-gather.9.cloned.1.call-done = f32[32,1200,64]{1,2,0:T(8,128)} async-done(((f32[1,1200,64]{1,2,0:T(8,128)}), f32[32,1200,64]{1,2,0:T(8,128)}) %all-gather.9.cloned.1.call-update) | async-done | bytes 9830416 | tf_op jit(solution)/shard_map/all_gather | solution.py:12
  674.1 6.1 cholesky.55
  686.9 10.6 %fusion.1 = bf16[64,16,4096]{2,0,1:T(8,128)(2,1)} fusion(bf16[64,16,4096]{2,0,1:T(8,128)(2,1)} %get-tuple-element.16, bf16[64,64,1]{1,0,2:T(8,128)(2,1)S(1)} %fusion.15, f32[16,4096]{1,0:T(8,128)S(1)} %broadcast_multiply_fusion.1), kind=kOutput, calls=%fused_computation.4 | convolution fusion | flops 562036736 | bytes 17047552 | tf_op jit(solution)/shard_map/dot_general | solution.py:83
  697.5 11.2 %copy.58 = bf16[64,16,4096]{2,1,0:T(8,128)(2,1)} copy(bf16[64,16,4096]{2,0,1:T(8,128)(2,1)} %fusion.1) | data formatting | bytes 16777216 | tf_op jit(solution)/shard_map/convert_element_type | solution.py:86
  708.7 99.7 %all_to_all.33 = bf16[64,16,4096]{2,1,0:T(8,128)(2,1)} all-to-all(bf16[64,16,4096]{2,1,0:T(8,128)(2,1)} %copy.58), channel_id=1, replica_groups=mesh['mem'=8,'pix'=4] {'mem'}, dimensions={0} | all-to-all | bytes 16777216 | tf_op jit(solution)/shard_map/all_to_all | solution.py:38
  808.4 7.9 copy.72
  (58 shorter events, 31.4 us)
Async XLA Ops:
  163.1 5.4 copy-start
  163.1 5.5 copy-start.2
  163.1 99.1 %all-to-all-start = ((bf16[8,2,262144]{2,1,0:T(2,128)(2,1)}), bf16[8,2,262144]{2,1,0:T(2,128)(2,1)}, u32[]{:S(2)}, u32[]{:S(2)}) async-start(bf16[8,2,262144]{2,1,0:T(2,128)(2,1)} %reshape.209), calls=%async_computation | async-start | bytes 16777216 | tf_op jit(solution)/shard_map/all_to_all | solution.py:33
  168.2 350.2 %all-gather.7.cloned.1.call-start = ((), (), s32[]{:S(2)}) async-start(), calls=%async_computation.2 | async-start | bytes 10813440 | tf_op jit(solution)/shard_map/all_gather | solution.py:12
  402.5 13.8 %copy-start.1 = (f32[1200]{0:T(1024)S(1)}, f32[1200]{0:T(1024)}, u32[]{:S(2)}) copy-start(f32[1200]{0:T(1024)} %param.11) | copy-start | bytes 14404
  415.9 252.3 %all-gather.9.cloned.1.call-start = ((), (), s32[]{:S(2)}) async-start(), calls=%async_computation.3 | async-start | bytes 10813440 | tf_op jit(solution)/shard_map/all_gather | solution.py:12
  480.2 27.1 %slice-start = ((s8[8388608]{0:T(1024)(128)(4,1)}), s8[4194304]{0:T(1024)(128)(4,1)S(1)}, s32[]{:S(2)}) async-start(s8[8388608]{0:T(1024)(128)(4,1)} %bitcast.113), calls=%async_computation.4 | async-start | bytes 8388608
  495.6 11.8 %slice-start.1 = ((s8[8388608]{0:T(1024)(128)(4,1)}), s8[4194304]{0:T(1024)(128)(4,1)S(1)}, s32[]{:S(2)}) async-start(s8[8388608]{0:T(1024)(128)(4,1)} %bitcast.113), calls=%async_computation.5 | async-start | bytes 8388608
  518.4 17.5 %copy-start.3 = (f32[2,1200,64]{1,2,0:T(8,128)S(1)}, f32[2,1200,64]{1,2,0:T(8,128)}, u32[]{:S(2)}) copy-start(f32[2,1200,64]{1,2,0:T(8,128)} %param.12) | copy-start | bytes 1843204
  518.4 17.5 %copy-start.4 = (f32[1200]{0:T(1024)S(1)}, f32[1200]{0:T(1024)}, u32[]{:S(2)}) copy-start(f32[1200]{0:T(1024)} %param.10) | copy-start | bytes 14404
Sparse Core Ops, SparseCore 0:
  416.0 85.2 all-gather.6
  582.5 85.6 all-gather.8
